TPU v7x, 32 devices: a whole 2x2x4 slice. The times are simulated.
32 devices in a mesh: row: 8 (over y, x, core), col: 4 (over z).
Axes of the slice: x: 2, y: 2, z: 4, core: 2. Of those that a mesh axis runs over, the one named last changes fastest.
Arguments:
- src_points: bfloat16 [8192, 256], P('row'), may hold values from -32 to 32, as said below
- tgt_points: bfloat16 [16384, 256], P(('col', 'row')), may hold values from -32 to 32, as said below
- log_src_mass: float32 [8192], P('row'), may hold values from -3 to 3
- log_tgt_mass: float32 [16384], P('col'), may hold values from -3 to 3
Outputs:
- src_potential: float32 [8192], P('row')
- tgt_potential: float32 [16384], P('col')
- mean_potentials: float32 [], replicated
Inputs may be any that keep to these rules, and one draw needn't show every extreme that they name: `src_points`: point coordinates. `tgt_points`: point coordinates.
All inputs are finite; a program needn't handle non-finite values.
Results may differ from a plain program's by a relative error of at most 0.0003.
Values may be sent and summed in bfloat16 or wider, within the bound.
A program may use at most 64 MiB of HBM per device.

v0:
```python
import jax
import jax.numpy as jnp
from jax import lax
from jax.sharding import PartitionSpec as P

ITERS = 3
entropy_weight = 0.1


def combined_all(value, axis, combine):
    everything = jax.tree.map(lambda part: lax.all_gather(part, axis), value)
    leading = jax.tree.map(lambda part: part[0], everything)

    def turn(k, so_far):
        return combine(so_far, jax.tree.map(lambda part: part[k], everything))

    return lax.fori_loop(1, lax.axis_size(axis), turn, leading)


def cost_block(points_a, squares_a, points_b, squares_b):
    product = lax.dot_general(
        points_a, points_b, (((1,), (1,)), ((), ())), preferred_element_type=jnp.float32
    )
    return (squares_a[:, None] + squares_b[None, :] - 2.0 * product) / points_a.shape[1]


def combine(early, later):
    top = jnp.maximum(early[0], later[0])
    return (top, early[1] * jnp.exp(early[0] - top) + later[1] * jnp.exp(later[0] - top))


def body(src_points, tgt_points, log_src_mass, log_tgt_mass):
    targets = lax.all_gather(tgt_points, "row", axis=0, tiled=True)
    sqy = jnp.sum(targets.astype(jnp.float32) ** 2, axis=1)
    count = src_points.shape[0]
    block = min(256, count)
    blocks = count // block
    src_blocks = src_points.reshape(blocks, block, -1)
    sq_blocks = jnp.sum(src_points.astype(jnp.float32) ** 2, axis=1).reshape(blocks, block)
    mass_blocks = log_src_mass.reshape(blocks, block)
    width_tgt = targets.shape[0]
    tgt_potential = jnp.zeros((width_tgt,), jnp.float32)
    src_potential = jnp.zeros((count,), jnp.float32)
    for step in range(ITERS):

        def row_terms(points, squares):
            cost = cost_block(points, squares, targets, sqy)
            return log_tgt_mass[None, :] + (tgt_potential[None, :] - cost) / entropy_weight

        def row_pair(item):
            terms = row_terms(item[0], item[1])
            top = jnp.max(terms, axis=1)
            return (top, jnp.sum(jnp.exp(terms - top[:, None]), axis=1))

        top, total = lax.map(row_pair, (src_blocks, sq_blocks))
        top, total = combined_all((top.reshape(-1), total.reshape(-1)), "col", combine)
        src_potential = -entropy_weight * (top + jnp.log(total))
        pot_blocks = src_potential.reshape(blocks, block)

        def col_terms(points, squares, mass, pot):
            cost = cost_block(points, squares, targets, sqy)
            return mass[:, None] + (pot[:, None] - cost) / entropy_weight

        def pair_step(carry, item):
            terms = col_terms(item[0], item[1], item[2], item[3])
            block_top = jnp.max(terms, axis=0)
            block_sum = jnp.sum(jnp.exp(terms - block_top[None, :]), axis=0)
            return (combine(carry, (block_top, block_sum)), None)

        start = (
            jnp.full((width_tgt,), -jnp.inf, jnp.float32),
            jnp.zeros((width_tgt,), jnp.float32),
        )
        inputs = (src_blocks, sq_blocks, mass_blocks, pot_blocks)
        (top, total), unused = lax.scan(pair_step, start, inputs)
        top, total = combined_all((top, total), "row", combine)
        tgt_potential = -entropy_weight * (top + jnp.log(total))
    sources_all = count * lax.axis_size("row")
    targets_all = width_tgt * lax.axis_size("col")
    local = jnp.sum(src_potential) / (sources_all * lax.axis_size("col")) + jnp.sum(
        tgt_potential
    ) / (targets_all * lax.axis_size("row"))
    mean_potentials = lax.psum(local, ("row", "col"))
    return (src_potential, tgt_potential, mean_potentials)


def solution(mesh):
    return jax.shard_map(
        body,
        mesh=mesh,
        in_specs=(P("row", None), P(("col", "row"), None), P("row"), P("col")),
        out_specs=(P("row"), P("col"), P()),
        check_vma=False,
    )
```

profile of v0, /device:TPU:0, one launch (start us, length us, event | category | flops | bytes accessed | tf_op | source)
XLA Modules:
  0.0 320.3 jit_solution(3803695196308315043)
XLA Ops:
  9.9 30.5 %all-gather.14.cloned.1.call-done = bf16[4096,256]{1,0:T(8,128)(2,1)} async-done(((bf16[512,256]{1,0:T(8,128)(2,1)}), bf16[4096,256]{1,0:T(8,128)(2,1)}) %all-gather.14.cloned.1.call-update) | async-done | bytes 2097168 | tf_op jit(solution)/shard_map/all_gather | solution.py:33
  42.6 15.6 %while.177 = (s32[]{:T(128)}, f32[4,256]{1,0:T(4,128)S(1)}, f32[4,256]{1,0:T(4,128)S(1)}, f32[4096]{0:T(1024)}, f32[4,256]{1,0:T(4,128)S(1)}, /*index=5*/f32[409...) while((s32[]{:T(128)}, f32[4,256]{1,0:T(4,128)S(1)}, ...), condition=%wide.region_5.6_spmd, body=%wide.region_2.5_spmd.sunk | while | flops 547356160 | bytes 10660465 | solution.py:55
  58.3 13.3 %all-gather.6 = f32[4,1,1024]{2,1,0:T(1,128)S(1)} all-gather(f32[1,1,1024]{2,1,0:T(1,128)S(1)} %reshape.89), channel_id=1, replica_groups=mesh['row'=8,'col'=4] {'col'}, dimensions={0}, use_global_device_ids=true | all-gather | bytes 20480 | tf_op jit(solution)/shard_map/all_gather | solution.py:11
  71.5 13.2 %all-gather.7 = f32[4,1,1024]{2,1,0:T(1,128)S(1)} all-gather(f32[1,1,1024]{2,1,0:T(1,128)S(1)} %reshape.91), channel_id=1, replica_groups=mesh['row'=8,'col'=4] {'col'}, dimensions={0}, use_global_device_ids=true | all-gather | bytes 20480 | tf_op jit(solution)/shard_map/all_gather | solution.py:11
  85.0 15.2 %while.186 = (s32[]{:T(128)}, f32[4096]{0:T(1024)S(1)}, f32[4096]{0:T(1024)S(1)}, f32[4,256]{1,0:T(4,128)S(1)}, f32[4,256]{1,0:T(4,128)S(1)}, /*index=5*/f32[4,2...) while((s32[]{:T(128)}, f32[4096]{0:T(1024)S(1)}, ...), condition=%wide.region_11.12_spmd.clone, body=%wide.region_8.11_spmd.clone.sunk | while | flops 547381248 | bytes 10790527 | solution.py:75
  85.0 3.1 fusion.87
  96.4 3.1 fusion.87
  100.2 9.2 %all-gather = f32[32768]{0:T(1024)S(1)} all-gather(f32[4096]{0:T(1024)S(1)} %get-tuple-element.1088), channel_id=2, replica_groups=mesh['row'=8,'col'=4] {'row'}, dimensions={0}, use_global_device_ids=true | all-gather | bytes 147456 | tf_op jit(solution)/shard_map/all_gather | solution.py:11
  109.4 8.3 %all-gather.1 = f32[32768]{0:T(1024)S(1)} all-gather(f32[4096]{0:T(1024)S(1)} %get-tuple-element.1089), channel_id=3, replica_groups=mesh['row'=8,'col'=4] {'row'}, dimensions={0}, use_global_device_ids=true | all-gather | bytes 147456 | tf_op jit(solution)/shard_map/all_gather | solution.py:11
  118.3 16.0 %while.180 = (s32[]{:T(128)}, f32[4,256]{1,0:T(4,128)S(1)}, f32[4,256]{1,0:T(4,128)S(1)}, f32[4096]{0:T(1024)S(1)}, f32[4096]{0:T(1024)S(1)}, /*index=5*/f32[4,2...) while((s32[]{:T(128)}, f32[4,256]{1,0:T(4,128)S(1)}, ...), condition=%wide.region_17.18_spmd, body=%wide.region_14.17_spmd.sunk | while | flops 547356160 | bytes 10676857 | solution.py:55
  118.4 3.2 fusion.83
  122.4 3.2 fusion.83
  126.4 3.2 fusion.83
  130.4 3.2 fusion.83
  134.4 13.2 %all-gather.8 = f32[4,1,1024]{2,1,0:T(1,128)S(1)} all-gather(f32[1,1,1024]{2,1,0:T(1,128)S(1)} %reshape.93), channel_id=1, replica_groups=mesh['row'=8,'col'=4] {'col'}, dimensions={0}, use_global_device_ids=true | all-gather | bytes 20480 | tf_op jit(solution)/shard_map/all_gather | solution.py:11
  147.6 13.2 %all-gather.9 = f32[4,1,1024]{2,1,0:T(1,128)S(1)} all-gather(f32[1,1,1024]{2,1,0:T(1,128)S(1)} %reshape.95), channel_id=1, replica_groups=mesh['row'=8,'col'=4] {'col'}, dimensions={0}, use_global_device_ids=true | all-gather | bytes 20480 | tf_op jit(solution)/shard_map/all_gather | solution.py:11
  161.0 15.2 %while.187 = (s32[]{:T(128)}, f32[4096]{0:T(1024)S(1)}, f32[4096]{0:T(1024)S(1)}, f32[4,256]{1,0:T(4,128)S(1)}, f32[4,256]{1,0:T(4,128)S(1)}, /*index=5*/f32[4,2...) while((s32[]{:T(128)}, f32[4096]{0:T(1024)S(1)}, ...), condition=%wide.region_23.24_spmd.clone, body=%wide.region_20.23_spmd.clone.sunk | while | flops 547381248 | bytes 10790527 | solution.py:75
  161.1 3.1 fusion.90
  176.2 9.3 %all-gather.2 = f32[32768]{0:T(1024)S(1)} all-gather(f32[4096]{0:T(1024)S(1)} %get-tuple-element.1096), channel_id=4, replica_groups=mesh['row'=8,'col'=4] {'row'}, dimensions={0}, use_global_device_ids=true | all-gather | bytes 147456 | tf_op jit(solution)/shard_map/all_gather | solution.py:11
  185.6 8.3 %all-gather.3 = f32[32768]{0:T(1024)S(1)} all-gather(f32[4096]{0:T(1024)S(1)} %get-tuple-element.1097), channel_id=5, replica_groups=mesh['row'=8,'col'=4] {'row'}, dimensions={0}, use_global_device_ids=true | all-gather | bytes 147456 | tf_op jit(solution)/shard_map/all_gather | solution.py:11
  194.5 16.0 %while.183 = (s32[]{:T(128)}, f32[4,256]{1,0:T(4,128)S(1)}, f32[4,256]{1,0:T(4,128)S(1)}, f32[4096]{0:T(1024)S(1)}, f32[4096]{0:T(1024)S(1)}, /*index=5*/f32[4,2...) while((s32[]{:T(128)}, f32[4,256]{1,0:T(4,128)S(1)}, ...), condition=%wide.region_29.30_spmd, body=%wide.region_26.29_spmd.sunk | while | flops 547356160 | bytes 10676857 | solution.py:55
  194.6 3.2 fusion.85
  198.6 3.2 fusion.85
  202.6 3.2 fusion.85
  206.6 3.2 fusion.85
  210.6 13.2 %all-gather.10 = f32[4,1,1024]{2,1,0:T(1,128)S(1)} all-gather(f32[1,1,1024]{2,1,0:T(1,128)S(1)} %reshape.97), channel_id=1, replica_groups=mesh['row'=8,'col'=4] {'col'}, dimensions={0}, use_global_device_ids=true | all-gather | bytes 20480 | tf_op jit(solution)/shard_map/all_gather | solution.py:11
  223.8 13.2 %all-gather.11 = f32[4,1,1024]{2,1,0:T(1,128)S(1)} all-gather(f32[1,1,1024]{2,1,0:T(1,128)S(1)} %reshape.99), channel_id=1, replica_groups=mesh['row'=8,'col'=4] {'col'}, dimensions={0}, use_global_device_ids=true | all-gather | bytes 20480 | tf_op jit(solution)/shard_map/all_gather | solution.py:11
  238.4 15.2 %while.188 = (s32[]{:T(128)}, f32[4096]{0:T(1024)S(1)}, f32[4096]{0:T(1024)S(1)}, f32[4,256]{1,0:T(4,128)S(1)}, f32[4,256]{1,0:T(4,128)S(1)}, /*index=5*/f32[4,2...) while((s32[]{:T(128)}, f32[4096]{0:T(1024)S(1)}, ...), condition=%wide.region_35.36_spmd.clone, body=%wide.region_32.35_spmd.clone.sunk | while | flops 547381248 | bytes 10790527 | solution.py:75
  246.0 3.1 fusion.93
  253.6 9.2 %all-gather.4 = f32[32768]{0:T(1024)S(1)} all-gather(f32[4096]{0:T(1024)S(1)} %get-tuple-element.1104), channel_id=6, replica_groups=mesh['row'=8,'col'=4] {'row'}, dimensions={0}, use_global_device_ids=true | all-gather | bytes 147456 | tf_op jit(solution)/shard_map/all_gather | solution.py:11
  262.8 8.3 %all-gather.5 = f32[32768]{0:T(1024)S(1)} all-gather(f32[4096]{0:T(1024)S(1)} %get-tuple-element.1105), channel_id=7, replica_groups=mesh['row'=8,'col'=4] {'row'}, dimensions={0}, use_global_device_ids=true | all-gather | bytes 147456 | tf_op jit(solution)/shard_map/all_gather | solution.py:11
  274.3 39.1 %psum.7 = f32[]{:T(128)} all-reduce(f32[]{:T(128)S(6)} %add.464), channel_id=1, replica_groups=mesh['row'=8,'col'=4] {'row','col'}, use_global_device_ids=true, to_apply=%region_40.41 | all-reduce | flops 1 | bytes 8 | tf_op jit(solution)/shard_map/psum | solution.py:83
  (235 shorter events, 65.7 us)
Async XLA Ops:
  7.2 33.2 %all-gather.14.cloned.1.call-start = ((), (), s32[]{:S(2)}) async-start(), calls=%async_computation | async-start | bytes 2359296 | tf_op jit(solution)/shard_map/all_gather | solution.py:33
  85.0 33.3 %copy-start.1 = (f32[4096]{0:T(1024)S(1)}, f32[4096]{0:T(1024)}, u32[]{:S(2)}) copy-start(f32[4096]{0:T(1024)} %get-tuple-element.2387) | copy-start | bytes 49156
  237.8 0.6 copy-start
Sparse Core Ops, SparseCore 0:
  9.9 30.4 all-gather.13
where the time goes:
time: 322 us; the launch traced here: 320 us
  blocking collectives  171 us (53%)
  matrix products  75.1 us (23%)
  waiting for transfers between devices  31.2 us (10%)
  other arithmetic  22 us (7%)
  between operations  15.7 us (5%)
  local copies, waits for them, and re-layouts  3.61 us (1%)
    all_gather x12, blocking collectives, combined_all(): everything = jax.tree.map(lambda part: lax.all_gather(part, axis), value)  132 us
    dot_general x24, matrix products, cost_block(): lax.dot_general(points_a, points_b, (((1,), (1,)), ((), ())), preferred_e...  75.1 us
    psum x1, blocking collectives, body(): mean_potentials = lax.psum(local, ('row', 'col'))  39.1 us
    all_gather x1, waiting for transfers between devices, body(): targets = lax.all_gather(tgt_points, 'row', axis=0, tiled=True)  30.5 us
    reduce_sum x12, other arithmetic, row_pair(): return (top, jnp.sum(jnp.exp(terms - top[:, None]), axis=1))  8.61 us
    reduce_sum x12, other arithmetic, pair_step(): block_sum = jnp.sum(jnp.exp(terms - block_top[None, :]), axis=0)  7.15 us
  transfers between devices with their start and end apart: 1, of which 1 were waited for; matrix products, arithmetic and copies ran while one was open for 1% of the time, Pallas kernels for 0%

commit v1 on v0

--- a/solution.py
+++ b/solution.py
@@ -30,7 +30,9 @@
 
 
 def body(src_points, tgt_points, log_src_mass, log_tgt_mass):
-    targets = lax.all_gather(tgt_points, "row", axis=0, tiled=True)
+    targets = jnp.concatenate(
+        lax.all_to_all(jnp.stack([tgt_points] * lax.axis_size("row")), "row", 0, 0), axis=0
+    )
     sqy = jnp.sum(targets.astype(jnp.float32) ** 2, axis=1)
     count = src_points.shape[0]
     block = min(256, count)

time: 322 us -> 268 us (0.83)
  matrix products: 75.1 us -> 35.4 us
  between operations: 15.7 us -> 2.4 us
  starting transfers between devices: 0.04 us -> 5.2 us
  waiting for transfers between devices: 31.2 us -> 26.3 us
    dot_general x24, matrix products: 75.1 us -> 35.4 us  [cost_block(): lax.dot_general(points_a, points_b, (((1,), (1,)), ((), ())), preferred_e...]
    all_gather x1 -> x0, waiting for transfers between devices: 30.5 us -> none  [body(): targets = lax.all_gather(tgt_points, 'row', axis=0, tiled=True)]
    all_to_all x0 -> x1, waiting for transfers between devices: none -> 26.3 us  [body(): lax.all_to_all(jnp.stack([tgt_points] * lax.axis_size('row')), 'row', 0, 0)]
    all_to_all x0 -> x1, starting transfers between devices: none -> 5.2 us  [body(): lax.all_to_all(jnp.stack([tgt_points] * lax.axis_size('row')), 'row', 0, 0)]
  transfers between devices with their start and end apart: 1 -> 1, of which waited for: 1 -> 1; matrix products, arithmetic and copies ran while one was open for 1% -> 0% of each run, Pallas kernels for 0% -> 0%
where the time goes in v1:
time: 268 us; the launch traced here: 267 us
  blocking collectives  171 us (64%)
  matrix products  35.4 us (13%)
  waiting for transfers between devices  26.3 us (10%)
  other arithmetic  19.3 us (7%)
  local copies, waits for them, and re-layouts  5.42 us (2%)
  starting transfers between devices  5.2 us (2%)
    all_gather x12, blocking collectives, combined_all(): everything = jax.tree.map(lambda part: lax.all_gather(part, axis), value)  132 us
    psum x1, blocking collectives, body(): mean_potentials = lax.psum(local, ('row', 'col'))  39.3 us
    dot_general x24, matrix products, cost_block(): lax.dot_general(points_a, points_b, (((1,), (1,)), ((), ())), preferred_e...  35.4 us
    all_to_all x1, waiting for transfers between devices, body(): lax.all_to_all(jnp.stack([tgt_points] * lax.axis_size('row')), 'row', 0, 0)  26.3 us
    reduce_sum x12, other arithmetic, row_pair(): return (top, jnp.sum(jnp.exp(terms - top[:, None]), axis=1))  8.61 us
    reduce_sum x12, other arithmetic, pair_step(): block_sum = jnp.sum(jnp.exp(terms - block_top[None, :]), axis=0)  7.15 us
  transfers between devices with their start and end apart: 1, of which 1 were waited for; matrix products, arithmetic and copies ran while one was open for 0% of the time, Pallas kernels for 0%

profile of v1, /device:TPU:0, one launch (start us, length us, event | category | flops | bytes accessed | tf_op | source)
XLA Modules:
  0.0 267.1 jit_solution(7850110872487817237)
XLA Ops:
  0.7 2.5 stack.2
  3.2 5.2 %all-to-all-start = ((bf16[8,512,256]{2,1,0:T(8,128)(2,1)}), bf16[8,512,256]{2,1,0:T(8,128)(2,1)S(1)}, u32[]{:S(2)}, u32[]{:S(2)}) async-start(bf16[8,512,256]{2,1,0:T(8,128)(2,1)} %stack.2), calls=%async_computation | async-start | bytes 4194304 | tf_op jit(solution)/shard_map/all_to_all | solution.py:34
  8.7 26.3 %all-to-all-done = bf16[8,512,256]{2,1,0:T(8,128)(2,1)S(1)} async-done(((bf16[8,512,256]{2,1,0:T(8,128)(2,1)}), bf16[8,512,256]{2,1,0:T(8,128)(2,1)S(1)}, u32[]{:S(2)}, u32[]{:S(2)}) %all-to-all-start) | async-done | bytes 2097184 | tf_op jit(solution)/shard_map/all_to_all | solution.py:34
  35.6 9.3 %while.177 = (s32[]{:T(128)}, f32[4,256]{1,0:T(4,128)S(1)}, f32[4,256]{1,0:T(4,128)S(1)}, f32[4096]{0:T(1024)S(1)}, f32[4,256]{1,0:T(4,128)S(1)}, /*index=5*/f32...) while((s32[]{:T(128)}, f32[4,256]{1,0:T(4,128)S(1)}, ...), condition=%wide.region_5.6_spmd, body=%wide.region_2.5_spmd.sunk | while | flops 547356160 | bytes 10659957 | solution.py:57
  38.0 1.5 fusion.81
  40.3 1.5 fusion.81
  44.9 13.4 %all-gather.6 = f32[4,1,1024]{2,1,0:T(1,128)S(1)} all-gather(f32[1,1,1024]{2,1,0:T(1,128)S(1)} %reshape.96), channel_id=1, replica_groups=mesh['row'=8,'col'=4] {'col'}, dimensions={0}, use_global_device_ids=true | all-gather | bytes 20480 | tf_op jit(solution)/shard_map/all_gather | solution.py:11
  58.4 13.2 %all-gather.7 = f32[4,1,1024]{2,1,0:T(1,128)S(1)} all-gather(f32[1,1,1024]{2,1,0:T(1,128)S(1)} %reshape.98), channel_id=1, replica_groups=mesh['row'=8,'col'=4] {'col'}, dimensions={0}, use_global_device_ids=true | all-gather | bytes 20480 | tf_op jit(solution)/shard_map/all_gather | solution.py:11
  71.8 8.5 %while.186 = (s32[]{:T(128)}, f32[4096]{0:T(1024)S(1)}, f32[4096]{0:T(1024)S(1)}, f32[4,256]{1,0:T(4,128)S(1)}, f32[4,256]{1,0:T(4,128)S(1)}, /*index=5*/f32[4,2...) while((s32[]{:T(128)}, f32[4096]{0:T(1024)S(1)}, ...), condition=%wide.region_11.12_spmd.clone, body=%wide.region_8.11_spmd.clone.sunk | while | flops 547381248 | bytes 10790019 | solution.py:77
  80.3 8.3 %all-gather = f32[32768]{0:T(1024)S(1)} all-gather(f32[4096]{0:T(1024)S(1)} %get-tuple-element.1088), channel_id=2, replica_groups=mesh['row'=8,'col'=4] {'row'}, dimensions={0}, use_global_device_ids=true | all-gather | bytes 147456 | tf_op jit(solution)/shard_map/all_gather | solution.py:11
  88.6 9.2 %all-gather.1 = f32[32768]{0:T(1024)S(1)} all-gather(f32[4096]{0:T(1024)S(1)} %get-tuple-element.1089), channel_id=3, replica_groups=mesh['row'=8,'col'=4] {'row'}, dimensions={0}, use_global_device_ids=true | all-gather | bytes 147456 | tf_op jit(solution)/shard_map/all_gather | solution.py:11
  98.5 9.4 %while.180 = (s32[]{:T(128)}, f32[4,256]{1,0:T(4,128)S(1)}, f32[4,256]{1,0:T(4,128)S(1)}, f32[4096]{0:T(1024)S(1)}, f32[4096]{0:T(1024)S(1)}, /*index=5*/f32[4,2...) while((s32[]{:T(128)}, f32[4,256]{1,0:T(4,128)S(1)}, ...), condition=%wide.region_17.18_spmd, body=%wide.region_14.17_spmd.sunk | while | flops 547356160 | bytes 10676349 | solution.py:57
  98.5 1.5 fusion.83
  100.8 1.5 fusion.83
  103.2 1.5 fusion.83
  105.5 1.5 fusion.83
  107.8 13.2 %all-gather.8 = f32[4,1,1024]{2,1,0:T(1,128)S(1)} all-gather(f32[1,1,1024]{2,1,0:T(1,128)S(1)} %reshape.100), channel_id=1, replica_groups=mesh['row'=8,'col'=4] {'col'}, dimensions={0}, use_global_device_ids=true | all-gather | bytes 20480 | tf_op jit(solution)/shard_map/all_gather | solution.py:11
  121.1 13.2 %all-gather.9 = f32[4,1,1024]{2,1,0:T(1,128)S(1)} all-gather(f32[1,1,1024]{2,1,0:T(1,128)S(1)} %reshape.102), channel_id=1, replica_groups=mesh['row'=8,'col'=4] {'col'}, dimensions={0}, use_global_device_ids=true | all-gather | bytes 20480 | tf_op jit(solution)/shard_map/all_gather | solution.py:11
  134.5 8.5 %while.187 = (s32[]{:T(128)}, f32[4096]{0:T(1024)S(1)}, f32[4096]{0:T(1024)S(1)}, f32[4,256]{1,0:T(4,128)S(1)}, f32[4,256]{1,0:T(4,128)S(1)}, /*index=5*/f32[4,2...) while((s32[]{:T(128)}, f32[4096]{0:T(1024)S(1)}, ...), condition=%wide.region_23.24_spmd.clone, body=%wide.region_20.23_spmd.clone.sunk | while | flops 547381248 | bytes 10790019 | solution.py:77
  143.0 8.4 %all-gather.2 = f32[32768]{0:T(1024)S(1)} all-gather(f32[4096]{0:T(1024)S(1)} %get-tuple-element.1096), channel_id=4, replica_groups=mesh['row'=8,'col'=4] {'row'}, dimensions={0}, use_global_device_ids=true | all-gather | bytes 147456 | tf_op jit(solution)/shard_map/all_gather | solution.py:11
  151.5 9.2 %all-gather.3 = f32[32768]{0:T(1024)S(1)} all-gather(f32[4096]{0:T(1024)S(1)} %get-tuple-element.1097), channel_id=5, replica_groups=mesh['row'=8,'col'=4] {'row'}, dimensions={0}, use_global_device_ids=true | all-gather | bytes 147456 | tf_op jit(solution)/shard_map/all_gather | solution.py:11
  161.3 9.4 %while.183 = (s32[]{:T(128)}, f32[4,256]{1,0:T(4,128)S(1)}, f32[4,256]{1,0:T(4,128)S(1)}, f32[4096]{0:T(1024)S(1)}, f32[4096]{0:T(1024)S(1)}, /*index=5*/f32[4,2...) while((s32[]{:T(128)}, f32[4,256]{1,0:T(4,128)S(1)}, ...), condition=%wide.region_29.30_spmd, body=%wide.region_26.29_spmd.sunk | while | flops 547356160 | bytes 10676349 | solution.py:57
  161.3 1.5 fusion.85
  163.7 1.5 fusion.85
  166.0 1.5 fusion.85
  168.4 1.5 fusion.85
  170.7 13.2 %all-gather.10 = f32[4,1,1024]{2,1,0:T(1,128)S(1)} all-gather(f32[1,1,1024]{2,1,0:T(1,128)S(1)} %reshape.104), channel_id=1, replica_groups=mesh['row'=8,'col'=4] {'col'}, dimensions={0}, use_global_device_ids=true | all-gather | bytes 20480 | tf_op jit(solution)/shard_map/all_gather | solution.py:11
  184.0 13.2 %all-gather.11 = f32[4,1,1024]{2,1,0:T(1,128)S(1)} all-gather(f32[1,1,1024]{2,1,0:T(1,128)S(1)} %reshape.106), channel_id=1, replica_groups=mesh['row'=8,'col'=4] {'col'}, dimensions={0}, use_global_device_ids=true | all-gather | bytes 20480 | tf_op jit(solution)/shard_map/all_gather | solution.py:11
  198.6 8.4 %while.188 = (s32[]{:T(128)}, f32[4096]{0:T(1024)S(1)}, f32[4096]{0:T(1024)S(1)}, f32[4,256]{1,0:T(4,128)S(1)}, f32[4,256]{1,0:T(4,128)S(1)}, /*index=5*/f32[4,2...) while((s32[]{:T(128)}, f32[4096]{0:T(1024)S(1)}, ...), condition=%wide.region_35.36_spmd.clone, body=%wide.region_32.35_spmd.clone.sunk | while | flops 547381248 | bytes 10790019 | solution.py:77
  207.0 8.3 %all-gather.4 = f32[32768]{0:T(1024)S(1)} all-gather(f32[4096]{0:T(1024)S(1)} %get-tuple-element.1104), channel_id=6, replica_groups=mesh['row'=8,'col'=4] {'row'}, dimensions={0}, use_global_device_ids=true | all-gather | bytes 147456 | tf_op jit(solution)/shard_map/all_gather | solution.py:11
  215.3 9.2 %all-gather.5 = f32[32768]{0:T(1024)S(1)} all-gather(f32[4096]{0:T(1024)S(1)} %get-tuple-element.1105), channel_id=7, replica_groups=mesh['row'=8,'col'=4] {'row'}, dimensions={0}, use_global_device_ids=true | all-gather | bytes 147456 | tf_op jit(solution)/shard_map/all_gather | solution.py:11
  227.8 39.3 %psum.7 = f32[]{:T(128)} all-reduce(f32[]{:T(128)S(6)} %add.464), channel_id=1, replica_groups=mesh['row'=8,'col'=4] {'row','col'}, use_global_device_ids=true, to_apply=%region_40.41 | all-reduce | flops 1 | bytes 8 | tf_op jit(solution)/shard_map/psum | solution.py:85
  (240 shorter events, 44.7 us)
Async XLA Ops:
  0.6 7.8 %copy-start = (bf16[1024,256]{1,0:T(8,128)(2,1)S(1)}, bf16[1024,256]{1,0:T(8,128)(2,1)}, u32[]{:S(2)}) copy-start(bf16[1024,256]{1,0:T(8,128)(2,1)} %param.28) | copy-start | bytes 1572868
  0.6 8.0 %copy-start.2 = (f32[1024]{0:T(1024)S(1)}, f32[1024]{0:T(1024)}, u32[]{:S(2)}) copy-start(f32[1024]{0:T(1024)} %param.30) | copy-start | bytes 12292
  0.7 35.0 %copy-start.3 = (f32[4096]{0:T(1024)S(1)}, f32[4096]{0:T(1024)}, u32[]{:S(2)}) copy-start(f32[4096]{0:T(1024)} %param.31) | copy-start | bytes 49156
  3.2 31.8 %all-to-all-start = ((bf16[8,512,256]{2,1,0:T(8,128)(2,1)}), bf16[8,512,256]{2,1,0:T(8,128)(2,1)S(1)}, u32[]{:S(2)}, u32[]{:S(2)}) async-start(bf16[8,512,256]{2,1,0:T(8,128)(2,1)} %stack.2), calls=%async_computation | async-start | bytes 4194304 | tf_op jit(solution)/shard_map/all_to_all | solution.py:34
  198.0 0.6 copy-start.1
